TPU v7x, 32 devices: a whole 2x2x4 slice. The times are simulated.
32 devices in a mesh: grp: 4 (over y, x), sub: 8 (over z, core).
Axes of the slice: x: 2, y: 2, z: 4, core: 2. Of those that a mesh axis runs over, the one named last changes fastest.
Arguments:
- bem_tiles: float32 [4096, 4096], P('grp', 'sub'), may hold values from -0.0625 to 0.0625
- leaf_inverse: float32 [4, 16, 1024, 1024], P('grp', 'sub'), may hold values from -1.5 to 1.5
- coupling: float32 [4, 16, 1024, 512], P('grp', 'sub'), may hold values from -0.0625 to 0.0625
- schur_inverse: float32 [4, 512, 512], P('grp', None, 'sub'), may hold values from -1.5 to 1.5
- leaf_load: float32 [4, 16, 1024, 128], P('grp', 'sub'), may hold values from -6 to 6
- sep_load: float32 [4, 512, 128], P('grp'), may hold values from -6 to 6
- surf_load: float32 [4096, 128], P(('grp', 'sub')), may hold values from -6 to 6
- surf_start: float32 [4096, 128], P(('grp', 'sub')), may hold values from -6 to 6
- flux_weight: float32 [4, 16, 8, 128], P('grp', 'sub'), may hold values from 0.25 to 1
- trace_weight: float32 [4, 16, 8, 128], P('grp', 'sub'), may hold values from 0.25 to 1
- leaf_sizes: int32 [4, 16], P('grp', 'sub'), may hold values from 512 to 1024
- block_counts: int32 [4, 16], P('grp', 'sub'), may hold values from 4 to 8
- block_owner: int32 [4, 16, 8, 1], P('grp', 'sub'), may hold values from 0 to 7; in each aligned block of 16 rows (0 to 15, 16 to 31, ..., all dimensions but the last counted through in order) at most 2 rows name the same one
Outputs:
- solution: float32 [4, 16, 1024, 128], P('grp', 'sub')
- sep_value: float32 [4, 512, 128], P('grp', 'sub')
- pressure: float32 [4096, 128], P(('grp', 'sub'))
Inputs may be any that keep to these rules, and one draw needn't show every extreme that they name: `block_owner`: of the 16 entries of one device, live or not, at most 2 name the same owner, and some device has 2 entries naming one owner.
All inputs are finite; a program needn't handle non-finite values.
Results may differ from a plain program's by a relative error of at most 0.00018.
Values sent between devices are 32-bit elements; how exact they have to be, the bound alone decides.
A program may use at most 128 MiB of HBM per device.

v0:
```python
import jax
import jax.numpy as jnp
from jax import lax
from jax.sharding import PartitionSpec as P

CAP = 2
SWEEPS = 3


def on_device(
    bem_tiles,
    leaf_inverse,
    coupling,
    schur_inverse,
    leaf_load,
    sep_load,
    surf_load,
    surf_start,
    flux_weight,
    trace_weight,
    leaf_sizes,
    block_counts,
    block_owner,
):
    highest = lax.Precision.HIGHEST
    parts = lax.axis_size("sub")
    here = lax.axis_index("sub")
    width = surf_load.shape[0]
    loads = surf_load.shape[1]
    leaves = leaf_inverse.shape[1]
    order = leaf_inverse.shape[2]
    blocks = order // width
    entries = leaves * blocks
    separator = schur_inverse.shape[1]
    sep_share = schur_inverse.shape[2]
    row_mask = (jnp.arange(order, dtype=jnp.int32)[None, :] < leaf_sizes[0][:, None]).astype(
        jnp.float32
    )[:, :, None]
    active = (
        (jnp.arange(blocks, dtype=jnp.int32)[None, :] < block_counts[0][:, None])
        .astype(jnp.float32)
        .reshape(entries)
    )
    owner = block_owner[0, :, :, 0].reshape(entries)
    picker = (owner[:, None] == jnp.arange(parts, dtype=jnp.int32)[None, :]).astype(jnp.float32)
    live_pick = picker * active[:, None]
    flux_scale = flux_weight[0].reshape(entries, width)[:, :, None]
    trace_scale = (trace_weight[0].reshape(entries, width) * active[:, None])[:, :, None]
    position = jnp.arange(entries, dtype=jnp.int32)
    earlier = (position[:, None] > position[None, :]) & (owner[:, None] == owner[None, :])
    slot_index = jnp.sum(earlier.astype(jnp.int32), axis=1)
    target = owner * CAP + slot_index
    placing = (jnp.arange(parts * CAP, dtype=jnp.int32)[:, None] == target[None, :]).astype(
        jnp.float32
    )
    schur_full = lax.all_gather(schur_inverse[0], "sub", axis=1, tiled=True)
    pressure = surf_start
    sep_value = jnp.zeros((separator, loads), jnp.float32)
    solution = jnp.zeros((leaves, order, loads), jnp.float32)
    for sweep in range(SWEEPS):
        column = lax.all_gather(pressure, "grp", axis=0, tiled=True)

        def tile_product(start, count, column=column):
            return jnp.dot(bem_tiles, column, precision=highest, preferred_element_type=jnp.float32)

        applied = lax.psum_scatter(
            tile_product(jnp.int32(0), lax.axis_size("sub") * width),
            "sub",
            scatter_dimension=0,
            tiled=True,
        )
        surface_patch = lax.all_gather(pressure, "sub", axis=0, tiled=True).reshape(
            parts, width, loads
        )
        flux = jnp.einsum("eo,oil->eil", live_pick, surface_patch, precision=highest) * flux_scale
        flux = flux.reshape(leaves, order, loads)
        pulled = jnp.einsum("jrs,sl->jrl", coupling[0], sep_value, precision=highest)
        rhs = (leaf_load[0] - pulled - flux) * row_mask
        solution = jnp.einsum("jrc,jcl->jrl", leaf_inverse[0], rhs, precision=highest) * row_mask
        partial_sum = jnp.einsum("jrs,jrl->sl", coupling[0], solution, precision=highest)
        summed = lax.psum(partial_sum, "sub")
        sep_value = jnp.dot(
            schur_full, sep_load[0] - summed, precision=highest, preferred_element_type=jnp.float32
        )
        weighted = solution.reshape(entries, width, loads) * trace_scale
        outgoing = jnp.dot(
            placing,
            weighted.reshape(entries, width * loads),
            precision=highest,
            preferred_element_type=jnp.float32,
        )
        incoming = lax.all_to_all(
            outgoing.reshape(parts, CAP, width, loads),
            "sub",
            split_axis=0,
            concat_axis=0,
            tiled=True,
        )
        trace = jnp.sum(incoming, axis=(0, 1))
        pressure = surf_load + applied + trace
    sep_rows_out = lax.dynamic_slice_in_dim(sep_value, here * sep_share, sep_share, 0)
    return (solution[None], sep_rows_out[None], pressure)


def solution(mesh):
    return jax.shard_map(
        on_device,
        mesh=mesh,
        in_specs=(
            P("grp", "sub"),
            P("grp", "sub", None, None),
            P("grp", "sub", None, None),
            P("grp", None, "sub"),
            P("grp", "sub", None, None),
            P("grp", None, None),
            P(("grp", "sub"), None),
            P(("grp", "sub"), None),
            P("grp", "sub", None, None),
            P("grp", "sub", None, None),
            P("grp", "sub"),
            P("grp", "sub"),
            P("grp", "sub", None, None),
        ),
        out_specs=(P("grp", "sub", None, None), P("grp", "sub", None), P(("grp", "sub"), None)),
        check_vma=False,
    )
```

profile of v0, /device:TPU:0, one launch (start us, length us, event | category | flops | bytes accessed | tf_op | source)
XLA Modules:
  0.0 464.7 jit_solution(11380869395240890339)
XLA Ops:
  7.3 10.9 %all_gather.23 = f32[512,128]{1,0:T(8,128)S(1)} all-gather(f32[128,128]{1,0:T(8,128)} %param.20), channel_id=1, replica_groups=mesh['grp'=4,'sub'=8] {'grp'}, dimensions={0}, use_global_device_ids=true | all-gather | bytes 327680 | tf_op jit(solution)/shard_map/all_gather | solution.py:61
  18.2 2.6 fusion.127
  20.8 15.6 %all_gather.21 = f32[1024,128]{1,0:T(8,128)S(1)} all-gather(f32[128,128]{1,0:T(8,128)} %param.20), channel_id=1, replica_groups=mesh['grp'=4,'sub'=8] {'sub'}, dimensions={0}, use_global_device_ids=true | all-gather | bytes 589824 | tf_op jit(solution)/shard_map/all_gather | solution.py:72
  39.7 1.3 copy.80
  41.0 1.6 copy.75
  42.6 7.2 %fusion.51 = f32[2,1024,128]{1,2,0:T(8,128)S(1)} fusion(f32[2,1024,128]{1,2,0:T(8,128)} %copy.80, f32[1,2,1024,512]{3,2,1,0:T(8,128)} %param.15, f32[1,2,1024,128]{2,3,1,0:T(8,128)S(1)} %copy.75, f32[2,1024]{1,0:T(2,128)S(1)} %compare_convert_fusion), kind=kOutput, calls=%fused_computation.29 | convolution fusion | flops 1611399168 | bytes 7348224 | tf_op jit(solution)/shard_map/jrs,sl->jrl/dot_general | solution.py:77
  49.8 12.1 %fusion.57 = f32[2,1024,128]{1,2,0:T(8,128)} fusion(f32[2,1024,128]{1,2,0:T(8,128)S(1)} %fusion.51, f32[1,2,1024,1024]{3,2,1,0:T(8,128)} %param.14, f32[2,1024]{1,0:T(2,128)S(1)} %compare_convert_fusion), kind=kOutput, calls=%fused_computation.34 | convolution fusion | flops 3221487616 | bytes 10493952 | tf_op jit(solution)/shard_map/jrc,jcl->jrl/dot_general | solution.py:79
  62.0 1.6 copy.81
  65.0 2.4 fusion.85
  68.7 5.2 %all-to-all-start = ((f32[8,2,128,128]{3,2,1,0:T(8,128)}), f32[8,2,128,128]{3,2,1,0:T(8,128)}, u32[]{:S(2)}, u32[]{:S(2)}) async-start(f32[8,2,128,128]{3,2,1,0:T(8,128)} %copy.83), calls=%async_computation.1 | async-start | bytes 2097152 | tf_op jit(solution)/shard_map/all_to_all | solution.py:92
  74.3 5.7 %fusion.69 = f32[512,128]{0,1:T(8,128)} fusion(f32[2,1024,128]{1,2,0:T(8,128)} %fusion.57, f32[1,2,1024,512]{3,2,1,0:T(8,128)} %param.15), kind=kOutput, calls=%fused_computation.40 | convolution fusion | flops 1610612736 | bytes 5505024 | tf_op jit(solution)/shard_map/jrs,jrl->sl/dot_general | solution.py:80
  81.8 20.1 %all-to-all-done = f32[8,2,128,128]{3,2,1,0:T(8,128)} async-done(((f32[8,2,128,128]{3,2,1,0:T(8,128)}), f32[8,2,128,128]{3,2,1,0:T(8,128)}, u32[]{:S(2)}, u32[]{:S(2)}) %all-to-all-start) | async-done | bytes 1048608 | tf_op jit(solution)/shard_map/all_to_all | solution.py:92
  101.9 1.9 reduce_sum.37
  104.8 14.8 %all_gather.24 = f32[1024,128]{1,0:T(8,128)S(1)} all-gather(f32[128,128]{1,0:T(8,128)S(1)} %add_add_fusion.2), channel_id=1, replica_groups=mesh['grp'=4,'sub'=8] {'sub'}, dimensions={0}, use_global_device_ids=true | all-gather | bytes 589824 | tf_op jit(solution)/shard_map/all_gather | solution.py:72
  119.5 1.8 convolution_multiply_fusion.1
  122.7 2.6 copy.86
  125.2 15.9 %all-reduce.4.cloned.1.call-done = f32[512,128]{0,1:T(8,128)} async-done(((f32[512,128]{0,1:T(8,128)}), f32[512,128]{0,1:T(8,128)}) %all-reduce.4.cloned.1.call-update) | async-done | bytes 262160 | tf_op jit(solution)/shard_map/psum | solution.py:81
  141.2 22.9 %all-gather.3.cloned.1.call-done = f32[1,512,512]{1,2,0:T(8,128)} async-done(((f32[1,512,64]{1,2,0:T(8,128)}), f32[1,512,512]{1,2,0:T(8,128)}) %all-gather.3.cloned.1.call-update) | async-done | bytes 1048592 | tf_op jit(solution)/shard_map/all_gather | solution.py:56
  164.1 2.0 convolution_bitcast_fusion.3
  166.1 7.2 %fusion.42 = f32[2,1024,128]{1,2,0:T(8,128)S(1)} fusion(f32[2,1024,128]{1,2,0:T(8,128)} %copy.86, f32[128,512,1]{1,0,2:T(8,128)S(1)} %convolution_bitcast_fusion.3, f32[1,2,1024,512]{3,2,1,0:T(8,128)} %param.15, f32[1,2,1024,128]{2,3,1,0:T(8,128)} %copy-done.2, f32[2,1024]{1,0:T(2,128)S(1)} %compare_convert_fusion), kind=kOutput, calls=%fused_computation.26 | convolution fusion | flops 1611399168 | bytes 7610368 | tf_op jit(solution)/shard_map/jrs,sl->jrl/dot_general | solution.py:77
  173.3 12.1 %fusion.63 = f32[2,1024,128]{1,2,0:T(8,128)} fusion(f32[2,1024,128]{1,2,0:T(8,128)S(1)} %fusion.42, f32[1,2,1024,1024]{3,2,1,0:T(8,128)} %param.14, f32[2,1024]{1,0:T(2,128)S(1)} %compare_convert_fusion), kind=kOutput, calls=%fused_computation.36 | convolution fusion | flops 3221487616 | bytes 10493952 | tf_op jit(solution)/shard_map/jrc,jcl->jrl/dot_general | solution.py:79
  185.4 2.6 copy.88
  188.0 2.4 reshape.166
  190.4 2.5 fusion.83
  194.0 4.2 all-to-all-start.1
  198.5 5.7 %fusion.72 = f32[512,128]{0,1:T(8,128)} fusion(f32[2,1024,128]{1,2,0:T(8,128)} %fusion.63, f32[1,2,1024,512]{3,2,1,0:T(8,128)} %param.15), kind=kOutput, calls=%fused_computation.41 | convolution fusion | flops 1610612736 | bytes 5505024 | tf_op jit(solution)/shard_map/jrs,jrl->sl/dot_general | solution.py:80
  204.2 9.0 %all_gather.25 = f32[512,128]{1,0:T(8,128)S(1)} all-gather(f32[128,128]{1,0:T(8,128)S(1)} %add_add_fusion.2), channel_id=1, replica_groups=mesh['grp'=4,'sub'=8] {'grp'}, dimensions={0}, use_global_device_ids=true | all-gather | bytes 327680 | tf_op jit(solution)/shard_map/all_gather | solution.py:61
  213.2 3.1 convolution_bitcast_fusion.1
  216.3 1.6 copy.87
  217.9 48.1 %all-reduce.6.cloned.1.call-done = f32[512,128]{0,1:T(8,128)} async-done(((f32[512,128]{0,1:T(8,128)}), f32[512,128]{0,1:T(8,128)}) %all-reduce.6.cloned.1.call-update) | async-done | bytes 262160 | tf_op jit(solution)/shard_map/psum | solution.py:81
  266.0 2.7 convolution_bitcast_fusion.2
  270.8 28.2 %reduce-scatter.6.cloned.1.call-done = f32[128,128]{0,1:T(8,128)} async-done(((f32[1024,128]{0,1:T(8,128)}), f32[128,128]{0,1:T(8,128)}) %reduce-scatter.6.cloned.1.call-update) | async-done | bytes 65552 | tf_op jit(solution)/shard_map/reduce_scatter | solution.py:66
  299.9 14.9 %all_gather.26 = f32[1024,128]{0,1:T(8,128)S(1)} all-gather(f32[128,128]{0,1:T(8,128)S(1)} %add_add_fusion.1), channel_id=1, replica_groups=mesh['grp'=4,'sub'=8] {'sub'}, dimensions={0}, use_global_device_ids=true | all-gather | bytes 589824 | tf_op jit(solution)/shard_map/all_gather | solution.py:72
  315.7 2.0 copy.93
  317.8 2.1 convolution_multiply_fusion
  321.1 2.6 copy.95
  323.7 7.2 %fusion.33 = f32[2,1024,128]{1,2,0:T(8,128)S(1)} fusion(f32[2,1024,128]{1,2,0:T(8,128)} %copy.95, f32[128,512,1]{1,0,2:T(8,128)} %convolution_bitcast_fusion.2, f32[1,2,1024,512]{3,2,1,0:T(8,128)} %param.15, f32[1,2,1024,128]{2,3,1,0:T(8,128)} %copy-done.2, f32[2,1024]{1,0:T(2,128)S(1)} %compare_convert_fusion), kind=kOutput, calls=%fused_computation.23 | convolution fusion | flops 1611399168 | bytes 7610368 | tf_op jit(solution)/shard_map/jrs,sl->jrl/dot_general | solution.py:77
  330.9 12.1 %fusion.66 = f32[2,128,1024]{2,1,0:T(8,128)} fusion(f32[2,1024,128]{1,2,0:T(8,128)S(1)} %fusion.33, f32[1,2,1024,1024]{3,2,1,0:T(8,128)} %param.14, f32[2,1024]{1,0:T(2,128)S(1)} %compare_convert_fusion), kind=kOutput, calls=%fused_computation.37 | convolution fusion | flops 3221487616 | bytes 10493952 | tf_op jit(solution)/shard_map/jrc,jcl->jrl/dot_general | solution.py:79
  343.0 2.6 copy.97
  345.7 2.4 reshape.169
  348.1 2.4 fusion.81
  351.7 4.2 all-to-all-start.2
  356.2 5.3 %fusion.75 = f32[512,128]{0,1:T(8,128)} fusion(f32[1,2,1024,512]{3,2,1,0:T(8,128)} %param.15, f32[2,128,1024]{2,1,0:T(8,128)S(1)} %copy-done.1), kind=kOutput, calls=%fused_computation.42 | convolution fusion | flops 1610612736 | bytes 5505024 | tf_op jit(solution)/shard_map/jrs,jrl->sl/dot_general | solution.py:80
  361.6 10.3 %all_gather.27 = f32[512,128]{0,1:T(8,128)S(1)} all-gather(f32[128,128]{0,1:T(8,128)S(1)} %add_add_fusion.1), channel_id=1, replica_groups=mesh['grp'=4,'sub'=8] {'grp'}, dimensions={0}, use_global_device_ids=true | all-gather | bytes 327680 | tf_op jit(solution)/shard_map/all_gather | solution.py:61
  371.9 3.1 convolution_bitcast_fusion
  376.3 47.2 %all-reduce.8.cloned.1.call-done = f32[512,128]{0,1:T(8,128)} async-done(((f32[512,128]{0,1:T(8,128)}), f32[512,128]{0,1:T(8,128)}) %all-reduce.8.cloned.1.call-update) | async-done | bytes 262160 | tf_op jit(solution)/shard_map/psum | solution.py:81
  423.6 3.1 fusion.87
  428.7 27.4 %reduce-scatter.8.cloned.1.call-done = f32[128,128]{0,1:T(8,128)} async-done(((f32[1024,128]{0,1:T(8,128)}), f32[128,128]{0,1:T(8,128)}) %reduce-scatter.8.cloned.1.call-update) | async-done | bytes 65552 | tf_op jit(solution)/shard_map/reduce_scatter | solution.py:66
  (73 shorter events, 23.6 us)
Async XLA Ops:
  7.2 11.0 %copy-start = (f32[1024,512]{1,0:T(8,128)S(1)}, f32[1024,512]{1,0:T(8,128)}, u32[]{:S(2)}) copy-start(f32[1024,512]{1,0:T(8,128)} %param.13) | copy-start | bytes 6291460
  7.2 29.7 %copy-start.9 = (s32[1,2,8,1]{2,3,1,0:T(1,128)S(1)}, s32[1,2,8,1]{2,3,1,0:T(1,128)}, u32[]{:S(2)}) copy-start(s32[1,2,8,1]{2,3,1,0:T(1,128)} %param.25) | copy-start | bytes 196
  7.2 30.6 %copy-start.11 = (s32[1,2]{1,0:T(1,128)S(1)}, s32[1,2]{1,0:T(1,128)}, u32[]{:S(2)}) copy-start(s32[1,2]{1,0:T(1,128)} %param.24) | copy-start | bytes 28
  7.2 30.8 %copy-start.10 = (s32[1,2]{1,0:T(1,128)S(1)}, s32[1,2]{1,0:T(1,128)}, u32[]{:S(2)}) copy-start(s32[1,2]{1,0:T(1,128)} %param.23) | copy-start | bytes 28
  7.2 30.8 %copy-start.4 = (f32[1,2,8,128]{3,2,1,0:T(8,128)S(1)}, f32[1,2,8,128]{3,2,1,0:T(8,128)}, u32[]{:S(2)}) copy-start(f32[1,2,8,128]{3,2,1,0:T(8,128)} %param.21) | copy-start | bytes 24580
  7.2 30.9 %copy-start.5 = (f32[1,2,8,128]{3,2,1,0:T(8,128)S(1)}, f32[1,2,8,128]{3,2,1,0:T(8,128)}, u32[]{:S(2)}) copy-start(f32[1,2,8,128]{3,2,1,0:T(8,128)} %param.22) | copy-start | bytes 24580
  7.2 96.6 %reduce-scatter.4.cloned.1.call-start = ((), (), s32[]{:S(2)}) async-start(), calls=%async_computation.7 | async-start | bytes 589824 | tf_op jit(solution)/shard_map/reduce_scatter | solution.py:66
  37.6 24.3 %copy-start.6 = (s32[16]{0:T(128)}, s32[16]{0:T(128)S(1)}, u32[]{:S(2)}) copy-start(s32[16]{0:T(128)S(1)} %eq.58) | copy-start | bytes 196
  42.6 19.3 %copy-start.2 = (f32[1,2,1024,128]{2,3,1,0:T(8,128)}, f32[1,2,1024,128]{2,3,1,0:T(8,128)S(1)}, u32[]{:S(2)}) copy-start(f32[1,2,1024,128]{2,3,1,0:T(8,128)S(1)} %copy.75) | copy-start | bytes 3145732
  61.9 5.5 %copy-start.7 = (s32[16]{0:T(128)}, s32[16]{0:T(128)S(1)}, u32[]{:S(2)}) copy-start(s32[16]{0:T(128)S(1)} %multiply_add_fusion.1) | copy-start | bytes 196
  68.7 33.3 %all-to-all-start = ((f32[8,2,128,128]{3,2,1,0:T(8,128)}), f32[8,2,128,128]{3,2,1,0:T(8,128)}, u32[]{:S(2)}, u32[]{:S(2)}) async-start(f32[8,2,128,128]{3,2,1,0:T(8,128)} %copy.83), calls=%async_computation.1 | async-start | bytes 2097152 | tf_op jit(solution)/shard_map/all_to_all | solution.py:92
  73.8 67.3 %all-reduce.4.cloned.1.call-start = ((), (), s32[]{:S(2)}) async-start(), calls=%async_computation.6 | async-start | bytes 524288 | tf_op jit(solution)/shard_map/psum | solution.py:81
  80.0 84.1 %all-gather.3.cloned.1.call-start = ((), (), s32[]{:S(2)}) async-start(), calls=%async_computation.12 | async-start | bytes 1179648 | tf_op jit(solution)/shard_map/all_gather | solution.py:56
  194.0 74.8 %all-to-all-start.1 = ((f32[8,2,128,128]{3,2,1,0:T(8,128)}), f32[8,2,128,128]{3,2,1,0:T(8,128)}, u32[]{:S(2)}, u32[]{:S(2)}) async-start(f32[8,2,128,128]{3,2,1,0:T(8,128)} %copy.90), calls=%async_computation.3 | async-start | bytes 2097152 | tf_op jit(solution)/shard_map/all_to_all | solution.py:92
  198.3 67.8 %all-reduce.6.cloned.1.call-start = ((), (), s32[]{:S(2)}) async-start(), calls=%async_computation.8 | async-start | bytes 524288 | tf_op jit(solution)/shard_map/psum | solution.py:81
  204.2 94.8 %reduce-scatter.6.cloned.1.call-start = ((), (), s32[]{:S(2)}) async-start(), calls=%async_computation.9 | async-start | bytes 589824 | tf_op jit(solution)/shard_map/reduce_scatter | solution.py:66
  343.0 5.0 %copy-start.8 = (s32[16]{0:T(128)S(1)}, s32[16]{0:T(128)}, u32[]{:S(2)}) copy-start(s32[16]{0:T(128)} %copy-done.7) | copy-start | bytes 196
  350.5 5.7 %copy-start.1 = (f32[2,128,1024]{2,1,0:T(8,128)S(1)}, f32[2,128,1024]{2,1,0:T(8,128)}, u32[]{:S(2)}) copy-start(f32[2,128,1024]{2,1,0:T(8,128)} %fusion.66) | copy-start | bytes 3145732
  351.7 75.6 %all-to-all-start.2 = ((f32[8,2,128,128]{3,2,1,0:T(8,128)}), f32[8,2,128,128]{3,2,1,0:T(8,128)}, u32[]{:S(2)}, u32[]{:S(2)}) async-start(f32[8,2,128,128]{3,2,1,0:T(8,128)} %copy.99), calls=%async_computation.5 | async-start | bytes 2097152 | tf_op jit(solution)/shard_map/all_to_all | solution.py:92
  356.0 67.6 %all-reduce.8.cloned.1.call-start = ((), (), s32[]{:S(2)}) async-start(), calls=%async_computation.10 | async-start | bytes 524288 | tf_op jit(solution)/shard_map/psum | solution.py:81
  361.6 94.5 %reduce-scatter.8.cloned.1.call-start = ((), (), s32[]{:S(2)}) async-start(), calls=%async_computation.11 | async-start | bytes 589824 | tf_op jit(solution)/shard_map/reduce_scatter | solution.py:66
  371.9 84.2 %copy-start.3 = (f32[128,128]{0,1:T(8,128)S(1)}, f32[128,128]{0,1:T(8,128)}, u32[]{:S(2)}) copy-start(f32[128,128]{0,1:T(8,128)} %copy.87) | copy-start | bytes 196612
Sparse Core Ops, SparseCore 0:
  20.9 31.6 reduce-scatter.3
  80.1 61.0 all-reduce.3
  142.8 21.2 all-gather.2
  204.3 61.7 all-reduce.5
  268.7 30.1 reduce-scatter.5
  361.7 61.8 all-reduce.7
  425.8 30.1 reduce-scatter.7
where the time goes:
time: 468 us; the launch traced here: 465 us
  waiting for transfers between devices  211 us (45%)
  matrix products  104 us (22%)
  blocking collectives  75.4 us (16%)
  local copies, waits for them, and re-layouts  37.4 us (8%)
  starting transfers between devices  14.7 us (3%)
  between operations  14.6 us (3%)
  other arithmetic  8.24 us (2%)
    psum x3, waiting for transfers between devices, on_device(): summed = lax.psum(partial_sum, 'sub')  111 us
    reduce_scatter x3, waiting for transfers between devices, on_device(): lax.psum_scatter(tile_product(jnp.int32(0), lax.axis_size('sub') * width)...  55.5 us
    all_gather x3, blocking collectives, on_device(): lax.all_gather(pressure, 'sub', axis=0, tiled=True)  45.3 us
    dot_general x3, matrix products, on_device(): jnp.einsum('jrc,jcl->jrl', leaf_inverse[0], rhs, precision=highest)  36.3 us
    all_gather x3, blocking collectives, on_device(): column = lax.all_gather(pressure, 'grp', axis=0, tiled=True)  30.1 us
    all_gather x1, waiting for transfers between devices, on_device(): schur_full = lax.all_gather(schur_inverse[0], 'sub', axis=1, tiled=True)  22.9 us
    dot_general x3, matrix products, on_device(): jnp.einsum('jrs,sl->jrl', coupling[0], sep_value, precision=highest)  21.6 us
    all_to_all x3, waiting for transfers between devices, on_device(): lax.all_to_all(outgoing.reshape(parts, CAP, width, loads), 'sub', split_a...  20.1 us
  transfers between devices with their start and end apart: 10, of which 7 were waited for; matrix products, arithmetic and copies ran while one was open for 17% of the time, Pallas kernels for 0%

commit v1 on v0

--- a/solution.py
+++ b/solution.py
@@ -78,7 +78,8 @@
         rhs = (leaf_load[0] - pulled - flux) * row_mask
         solution = jnp.einsum("jrc,jcl->jrl", leaf_inverse[0], rhs, precision=highest) * row_mask
         partial_sum = jnp.einsum("jrs,jrl->sl", coupling[0], solution, precision=highest)
-        summed = lax.psum(partial_sum, "sub")
+        terms = lax.all_gather(partial_sum, "sub", axis=0, tiled=False)
+        summed = terms.sum(axis=0)
         sep_value = jnp.dot(
             schur_full, sep_load[0] - summed, precision=highest, preferred_element_type=jnp.float32
         )

time: 468 us -> 382 us (0.82)
  waiting for transfers between devices: 211 us -> 115 us
  local copies, waits for them, and re-layouts: 37.4 us -> 52 us
  matrix products: 104 us -> 89.5 us
    psum x3 -> x0, waiting for transfers between devices: 111 us -> none  [on_device(): summed = lax.psum(partial_sum, 'sub')]
    all_to_all x3, waiting for transfers between devices: 20.1 us -> 114 us  [on_device(): lax.all_to_all(outgoing.reshape(parts, CAP, width, loads), 'sub', split_a...]
    reduce_scatter x3, waiting for transfers between devices: 55.5 us -> 0.01 us  [on_device(): lax.psum_scatter(tile_product(jnp.int32(0), lax.axis_size('sub') * width)...]
    all_gather x1, waiting for transfers between devices: 22.9 us -> 0.01 us  [on_device(): schur_full = lax.all_gather(schur_inverse[0], 'sub', axis=1, tiled=True)]
    unnamed x31 -> x56, local copies, waits for them, and re-layouts: 7.7 us -> 19.7 us
    dot_general x3, matrix products: 16.6 us -> 9.48 us  [on_device(): jnp.einsum('jrs,jrl->sl', coupling[0], solution, precision=highest)]
  transfers between devices with their start and end apart: 10 -> 10, of which waited for: 7 -> 3; matrix products, arithmetic and copies ran while one was open for 17% -> 37% of each run, Pallas kernels for 0% -> 0%
where the time goes in v1:
time: 382 us; the launch traced here: 375 us
  waiting for transfers between devices  115 us (30%)
  matrix products  89.5 us (23%)
  blocking collectives  78.4 us (21%)
  local copies, waits for them, and re-layouts  52 us (14%)
  between operations  15.1 us (4%)
  starting transfers between devices  14.3 us (4%)
  other arithmetic  10.6 us (3%)
    all_to_all x3, waiting for transfers between devices, on_device(): lax.all_to_all(outgoing.reshape(parts, CAP, width, loads), 'sub', split_a...  114 us
    all_gather x3, blocking collectives, on_device(): lax.all_gather(pressure, 'sub', axis=0, tiled=True)  47.7 us
    dot_general x3, matrix products, on_device(): jnp.einsum('jrc,jcl->jrl', leaf_inverse[0], rhs, precision=highest)  34.2 us
    all_gather x3, blocking collectives, on_device(): column = lax.all_gather(pressure, 'grp', axis=0, tiled=True)  30.8 us
    unnamed x56, local copies, waits for them, and re-layouts  19.7 us
    dot_general x3, matrix products, on_device(): jnp.einsum('jrs,sl->jrl', coupling[0], sep_value, precision=highest)  18.9 us
    all_to_all x3, starting transfers between devices, on_device(): lax.all_to_all(outgoing.reshape(parts, CAP, width, loads), 'sub', split_a...  14.1 us
    dot_general x3, matrix products, on_device(): jnp.einsum('jrs,jrl->sl', coupling[0], solution, precision=highest)  9.48 us
  transfers between devices with their start and end apart: 10, of which 3 were waited for; matrix products, arithmetic and copies ran while one was open for 37% of the time, Pallas kernels for 0%

profile of v1, /device:TPU:0, one launch (start us, length us, event | category | flops | bytes accessed | tf_op | source)
XLA Modules:
  0.0 375.0 jit_solution(15609165641557830710)
XLA Ops:
  7.3 10.9 %all_gather.43 = f32[512,128]{1,0:T(8,128)S(1)} all-gather(f32[128,128]{1,0:T(8,128)} %param.20), channel_id=1, replica_groups=mesh['grp'=4,'sub'=8] {'grp'}, dimensions={0}, use_global_device_ids=true | all-gather | bytes 327680 | tf_op jit(solution)/shard_map/all_gather | solution.py:61
  18.1 2.6 fusion.127
  20.8 16.3 %all_gather.39 = f32[1024,128]{1,0:T(8,128)} all-gather(f32[128,128]{1,0:T(8,128)} %param.20), channel_id=1, replica_groups=mesh['grp'=4,'sub'=8] {'sub'}, dimensions={0}, use_global_device_ids=true | all-gather | bytes 589824 | tf_op jit(solution)/shard_map/all_gather | solution.py:72
  38.6 2.2 convolution_multiply_fusion.2
  42.1 2.5 copy.80
  44.8 1.6 copy.75
  46.3 7.2 %fusion.51 = f32[2,1024,128]{1,2,0:T(8,128)S(1)} fusion(f32[2,1024,128]{1,2,0:T(8,128)} %copy.80, f32[1,2,1024,512]{3,2,1,0:T(8,128)} %param.15, f32[1,2,1024,128]{2,3,1,0:T(8,128)S(1)} %copy.75, f32[2,1024]{1,0:T(2,128)S(1)} %compare_convert_fusion), kind=kOutput, calls=%fused_computation.32 | convolution fusion | flops 1611399168 | bytes 7348224 | tf_op jit(solution)/shard_map/jrs,sl->jrl/dot_general | solution.py:77
  53.6 11.4 %fusion.57 = f32[2,1024,128]{1,2,0:T(8,128)S(1)} fusion(f32[2,1024,128]{1,2,0:T(8,128)S(1)} %fusion.51, f32[1,2,1024,1024]{3,2,1,0:T(8,128)} %param.14, f32[2,1024]{1,0:T(2,128)S(1)} %compare_convert_fusion), kind=kOutput, calls=%fused_computation.37 | convolution fusion | flops 3221487616 | bytes 10493952 | tf_op jit(solution)/shard_map/jrc,jcl->jrl/dot_general | solution.py:79
  66.0 3.2 fusion.69
  69.2 1.6 copy.81
  72.6 2.4 fusion.85
  76.2 5.3 %all-to-all-start = ((f32[8,2,128,128]{3,2,1,0:T(8,128)}), f32[8,2,128,128]{3,2,1,0:T(8,128)}, u32[]{:S(2)}, u32[]{:S(2)}) async-start(f32[8,2,128,128]{3,2,1,0:T(8,128)} %copy.83), calls=%async_computation.1 | async-start | bytes 2097152 | tf_op jit(solution)/shard_map/all_to_all | solution.py:93
  83.3 37.0 %all-to-all-done = f32[8,2,128,128]{3,2,1,0:T(8,128)} async-done(((f32[8,2,128,128]{3,2,1,0:T(8,128)}), f32[8,2,128,128]{3,2,1,0:T(8,128)}, u32[]{:S(2)}, u32[]{:S(2)}) %all-to-all-start) | async-done | bytes 1048608 | tf_op jit(solution)/shard_map/all_to_all | solution.py:93
  120.3 1.9 reduce_sum.65
  123.2 16.6 %all_gather.44 = f32[1024,128]{1,0:T(8,128)S(1)} all-gather(f32[128,128]{1,0:T(8,128)S(1)} %add_add_fusion.2), channel_id=1, replica_groups=mesh['grp'=4,'sub'=8] {'sub'}, dimensions={0}, use_global_device_ids=true | all-gather | bytes 589824 | tf_op jit(solution)/shard_map/all_gather | solution.py:72
  139.7 1.8 convolution_multiply_fusion.1
  142.8 2.5 copy.86
  145.3 9.4 %all_gather.47 = f32[512,128]{1,0:T(8,128)S(1)} all-gather(f32[128,128]{1,0:T(8,128)S(1)} %add_add_fusion.2), channel_id=1, replica_groups=mesh['grp'=4,'sub'=8] {'grp'}, dimensions={0}, use_global_device_ids=true | all-gather | bytes 327680 | tf_op jit(solution)/shard_map/all_gather | solution.py:61
  154.7 3.2 convolution_bitcast_fusion.1
  158.0 3.2 copy.110
  162.5 2.0 convolution_bitcast_fusion.3
  164.5 7.2 %fusion.42 = f32[2,1024,128]{1,2,0:T(8,128)S(1)} fusion(f32[2,1024,128]{1,2,0:T(8,128)} %copy.86, f32[128,512,1]{1,0,2:T(8,128)S(1)} %convolution_bitcast_fusion.3, f32[1,2,1024,512]{3,2,1,0:T(8,128)} %param.15, f32[1,2,1024,128]{2,3,1,0:T(8,128)} %copy-done.6, f32[2,1024]{1,0:T(2,128)S(1)} %compare_convert_fusion), kind=kOutput, calls=%fused_computation.29 | convolution fusion | flops 1611399168 | bytes 7610368 | tf_op jit(solution)/shard_map/jrs,sl->jrl/dot_general | solution.py:77
  171.7 11.4 %fusion.63 = f32[2,1024,128]{1,2,0:T(8,128)S(1)} fusion(f32[2,1024,128]{1,2,0:T(8,128)S(1)} %fusion.42, f32[1,2,1024,1024]{3,2,1,0:T(8,128)} %param.14, f32[2,1024]{1,0:T(2,128)S(1)} %compare_convert_fusion), kind=kOutput, calls=%fused_computation.39 | convolution fusion | flops 3221487616 | bytes 10493952 | tf_op jit(solution)/shard_map/jrc,jcl->jrl/dot_general | solution.py:79
  184.1 3.2 fusion.72
  187.3 2.5 copy.88
  189.8 2.4 reshape.166
  192.2 2.5 fusion.83
  195.9 4.2 %all-to-all-start.1 = ((f32[8,2,128,128]{3,2,1,0:T(8,128)}), f32[8,2,128,128]{3,2,1,0:T(8,128)}, u32[]{:S(2)}, u32[]{:S(2)}) async-start(f32[8,2,128,128]{3,2,1,0:T(8,128)} %copy.90), calls=%async_computation.3 | async-start | bytes 2097152 | tf_op jit(solution)/shard_map/all_to_all | solution.py:93
  200.9 36.7 %all-to-all-done.1 = f32[8,2,128,128]{3,2,1,0:T(8,128)} async-done(((f32[8,2,128,128]{3,2,1,0:T(8,128)}), f32[8,2,128,128]{3,2,1,0:T(8,128)}, u32[]{:S(2)}, u32[]{:S(2)}) %all-to-all-start.1) | async-done | bytes 1048608 | tf_op jit(solution)/shard_map/all_to_all | solution.py:93
  240.6 14.8 %all_gather.48 = f32[1024,128]{0,1:T(8,128)S(1)} all-gather(f32[128,128]{0,1:T(8,128)S(1)} %add_add_fusion.1), channel_id=1, replica_groups=mesh['grp'=4,'sub'=8] {'sub'}, dimensions={0}, use_global_device_ids=true | all-gather | bytes 589824 | tf_op jit(solution)/shard_map/all_gather | solution.py:72
  256.3 2.0 copy.93
  258.3 2.1 convolution_multiply_fusion
  260.4 1.3 copy.94
  261.7 2.5 copy.95
  264.3 10.5 %all_gather.51 = f32[512,128]{0,1:T(8,128)S(1)} all-gather(f32[128,128]{0,1:T(8,128)S(1)} %add_add_fusion.1), channel_id=1, replica_groups=mesh['grp'=4,'sub'=8] {'grp'}, dimensions={0}, use_global_device_ids=true | all-gather | bytes 327680 | tf_op jit(solution)/shard_map/all_gather | solution.py:61
  274.7 3.1 convolution_bitcast_fusion
  278.0 3.4 copy.112
  282.8 4.5 %fusion.33 = f32[2,1024,128]{1,2,0:T(8,128)S(1)} fusion(f32[2,1024,128]{1,2,0:T(8,128)S(1)} %copy-done.12, f32[128,512,1]{1,0,2:T(8,128)S(1)} %convolution_bitcast_fusion.2, f32[1,2,1024,512]{3,2,1,0:T(8,128)S(1)} %copy-done.3, f32[1,2,1024,128]{2,3,1,0:T(8,128)S(1)} %copy-done.7, f32[2,1024]{1,0:T(2,128)S(1)} %compare_convert_fusion), kind=kOutput, calls=%fused_computation.26 | convolution fusion | flops 1611399168 | bytes 7610368 | tf_op jit(solution)/shard_map/jrs,sl->jrl/dot_general | solution.py:77
  287.2 11.4 %fusion.66 = f32[2,128,1024]{2,1,0:T(8,128)S(1)} fusion(f32[2,1024,128]{1,2,0:T(8,128)S(1)} %fusion.33, f32[1,2,1024,1024]{3,2,1,0:T(8,128)} %param.14, f32[2,1024]{1,0:T(2,128)S(1)} %compare_convert_fusion), kind=kOutput, calls=%fused_computation.40 | convolution fusion | flops 3221487616 | bytes 10493952 | tf_op jit(solution)/shard_map/jrc,jcl->jrl/dot_general | solution.py:79
  299.6 3.2 fusion.75
  302.8 2.6 copy.97
  305.3 2.4 reshape.169
  307.7 2.4 fusion.81
  311.4 4.6 %all-to-all-start.2 = ((f32[8,2,128,128]{3,2,1,0:T(8,128)}), f32[8,2,128,128]{3,2,1,0:T(8,128)}, u32[]{:S(2)}, u32[]{:S(2)}) async-start(f32[8,2,128,128]{3,2,1,0:T(8,128)} %copy.99), calls=%async_computation.5 | async-start | bytes 2097152 | tf_op jit(solution)/shard_map/all_to_all | solution.py:93
  315.9 1.3 copy.102
  317.3 40.5 %all-to-all-done.2 = f32[8,2,128,128]{3,2,1,0:T(8,128)} async-done(((f32[8,2,128,128]{3,2,1,0:T(8,128)}), f32[8,2,128,128]{3,2,1,0:T(8,128)}, u32[]{:S(2)}, u32[]{:S(2)}) %all-to-all-start.2) | async-done | bytes 1048608 | tf_op jit(solution)/shard_map/all_to_all | solution.py:93
  361.4 3.2 copy.114
  365.2 1.8 fusion.87
  (101 shorter events, 27.4 us)
Async XLA Ops:
  7.2 11.0 %copy-start = (f32[1024,512]{1,0:T(8,128)S(1)}, f32[1024,512]{1,0:T(8,128)}, u32[]{:S(2)}) copy-start(f32[1024,512]{1,0:T(8,128)} %param.13) | copy-start | bytes 6291460
  7.2 30.5 %copy-start.20 = (s32[1,2,8,1]{2,3,1,0:T(1,128)S(1)}, s32[1,2,8,1]{2,3,1,0:T(1,128)}, u32[]{:S(2)}) copy-start(s32[1,2,8,1]{2,3,1,0:T(1,128)} %param.25) | copy-start | bytes 196
  7.2 31.2 %copy-start.22 = (s32[1,2]{1,0:T(1,128)S(1)}, s32[1,2]{1,0:T(1,128)}, u32[]{:S(2)}) copy-start(s32[1,2]{1,0:T(1,128)} %param.24) | copy-start | bytes 28
  7.2 31.3 %copy-start.15 = (f32[1,2,8,128]{3,2,1,0:T(8,128)S(1)}, f32[1,2,8,128]{3,2,1,0:T(8,128)}, u32[]{:S(2)}) copy-start(f32[1,2,8,128]{3,2,1,0:T(8,128)} %param.21) | copy-start | bytes 24580
  7.2 115.0 %reduce-scatter.4.cloned.1.call-start = ((), (), s32[]{:S(2)}) async-start(), calls=%async_computation.6 | async-start | bytes 589824 | tf_op jit(solution)/shard_map/reduce_scatter | solution.py:66
  20.8 23.9 %copy-start.21 = (s32[1,2]{1,0:T(1,128)S(1)}, s32[1,2]{1,0:T(1,128)}, u32[]{:S(2)}) copy-start(s32[1,2]{1,0:T(1,128)} %param.23) | copy-start | bytes 28
  20.8 137.2 %all-gather.9.cloned.1.call-start = ((), (), s32[]{:S(2)}) async-start(), calls=%async_computation.9 | async-start | bytes 2359296 | tf_op jit(solution)/shard_map/all_gather | solution.py:81
  38.4 33.8 %copy-start.19 = (s32[16]{0:T(128)}, s32[16]{0:T(128)S(1)}, u32[]{:S(2)}) copy-start(s32[16]{0:T(128)S(1)} %eq.58) | copy-start | bytes 196
  46.3 18.7 %copy-start.6 = (f32[1,2,1024,128]{2,3,1,0:T(8,128)}, f32[1,2,1024,128]{2,3,1,0:T(8,128)S(1)}, u32[]{:S(2)}) copy-start(f32[1,2,1024,128]{2,3,1,0:T(8,128)S(1)} %copy.75) | copy-start | bytes 3145732
  53.6 12.4 %copy-start.1 = (f32[1,2,1024,512]{3,2,1,0:T(8,128)S(1)}, f32[1,2,1024,512]{3,2,1,0:T(8,128)}, u32[]{:S(2)}) copy-start(f32[1,2,1024,512]{3,2,1,0:T(8,128)} %param.15) | copy-start | bytes 12582916
  65.1 1.0 copy-start.10
  66.0 6.1 %copy-start.16 = (f32[1,2,8,128]{3,2,1,0:T(8,128)S(1)}, f32[1,2,8,128]{3,2,1,0:T(8,128)}, u32[]{:S(2)}) copy-start(f32[1,2,8,128]{3,2,1,0:T(8,128)} %param.22) | copy-start | bytes 24580
  72.2 4.0 %copy-start.17 = (s32[16]{0:T(128)}, s32[16]{0:T(128)S(1)}, u32[]{:S(2)}) copy-start(s32[16]{0:T(128)S(1)} %multiply_add_fusion.1) | copy-start | bytes 196
  76.2 44.1 %all-to-all-start = ((f32[8,2,128,128]{3,2,1,0:T(8,128)}), f32[8,2,128,128]{3,2,1,0:T(8,128)}, u32[]{:S(2)}, u32[]{:S(2)}) async-start(f32[8,2,128,128]{3,2,1,0:T(8,128)} %copy.83), calls=%async_computation.1 | async-start | bytes 2097152 | tf_op jit(solution)/shard_map/all_to_all | solution.py:93
  81.5 81.0 %all-gather.11.cloned.1.call-start = ((), (), s32[]{:S(2)}) async-start(), calls=%async_computation.10 | async-start | bytes 1179648 | tf_op jit(solution)/shard_map/all_gather | solution.py:56
  82.2 157.5 %reduce-scatter.6.cloned.1.call-start = ((), (), s32[]{:S(2)}) async-start(), calls=%async_computation.7 | async-start | bytes 589824 | tf_op jit(solution)/shard_map/reduce_scatter | solution.py:66
  157.9 120.0 %all-gather.13.cloned.1.call-start = ((), (), s32[]{:S(2)}) async-start(), calls=%async_computation.11 | async-start | bytes 2359296 | tf_op jit(solution)/shard_map/all_gather | solution.py:81
  171.7 12.4 %copy-start.2 = (f32[1,2,1024,512]{3,2,1,0:T(8,128)S(1)}, f32[1,2,1024,512]{3,2,1,0:T(8,128)}, u32[]{:S(2)}) copy-start(f32[1,2,1024,512]{3,2,1,0:T(8,128)} %param.15) | copy-start | bytes 12582916
  183.1 1.0 copy-start.11
  192.2 8.0 %copy-start.14 = (f32[128,128]{1,0:T(8,128)S(1)}, f32[128,128]{1,0:T(8,128)}, u32[]{:S(2)}) copy-start(f32[128,128]{1,0:T(8,128)} %param.19) | copy-start | bytes 196612
  195.9 41.7 %all-to-all-start.1 = ((f32[8,2,128,128]{3,2,1,0:T(8,128)}), f32[8,2,128,128]{3,2,1,0:T(8,128)}, u32[]{:S(2)}, u32[]{:S(2)}) async-start(f32[8,2,128,128]{3,2,1,0:T(8,128)} %copy.90), calls=%async_computation.3 | async-start | bytes 2097152 | tf_op jit(solution)/shard_map/all_to_all | solution.py:93
  200.1 159.7 %reduce-scatter.8.cloned.1.call-start = ((), (), s32[]{:S(2)}) async-start(), calls=%async_computation.8 | async-start | bytes 589824 | tf_op jit(solution)/shard_map/reduce_scatter | solution.py:66
  277.9 83.6 %all-gather.15.cloned.1.call-start = ((), (), s32[]{:S(2)}) async-start(), calls=%async_computation.12 | async-start | bytes 2359296 | tf_op jit(solution)/shard_map/all_gather | solution.py:81
  277.9 4.1 %copy-start.8 = (f32[1,512,512]{1,2,0:T(8,128)S(1)}, f32[1,512,512]{1,2,0:T(8,128)}, u32[]{:S(2)}) copy-start(f32[1,512,512]{1,2,0:T(8,128)} %all-gather.11.cloned.1.call-done) | copy-start | bytes 3145732
  277.9 4.8 %copy-start.3 = (f32[1,2,1024,512]{3,2,1,0:T(8,128)S(1)}, f32[1,2,1024,512]{3,2,1,0:T(8,128)}, u32[]{:S(2)}) copy-start(f32[1,2,1024,512]{3,2,1,0:T(8,128)} %param.15) | copy-start | bytes 12582916
  278.0 4.8 %copy-start.7 = (f32[1,2,1024,128]{2,3,1,0:T(8,128)S(1)}, f32[1,2,1024,128]{2,3,1,0:T(8,128)}, u32[]{:S(2)}) copy-start(f32[1,2,1024,128]{2,3,1,0:T(8,128)} %copy-done.6) | copy-start | bytes 3145732
  278.0 4.8 %copy-start.12 = (f32[2,1024,128]{1,2,0:T(8,128)S(1)}, f32[2,1024,128]{1,2,0:T(8,128)}, u32[]{:S(2)}) copy-start(f32[2,1024,128]{1,2,0:T(8,128)} %copy.95) | copy-start | bytes 3145732
  298.6 1.0 copy-start.4
  299.6 8.2 %copy-start.18 = (s32[16]{0:T(128)S(1)}, s32[16]{0:T(128)}, u32[]{:S(2)}) copy-start(s32[16]{0:T(128)} %copy-done.17) | copy-start | bytes 196
  310.2 5.8 %copy-start.5 = (f32[2,128,1024]{2,1,0:T(8,128)S(1)}, f32[2,128,1024]{2,1,0:T(8,128)}, u32[]{:S(2)}) copy-start(f32[2,128,1024]{2,1,0:T(8,128)} %copy-done.4) | copy-start | bytes 3145732
  310.2 49.6 %copy-start.13 = (f32[128,128]{0,1:T(8,128)S(1)}, f32[128,128]{0,1:T(8,128)}, u32[]{:S(2)}) copy-start(f32[128,128]{0,1:T(8,128)} %copy.87) | copy-start | bytes 196612
  311.4 46.4 %all-to-all-start.2 = ((f32[8,2,128,128]{3,2,1,0:T(8,128)}), f32[8,2,128,128]{3,2,1,0:T(8,128)}, u32[]{:S(2)}, u32[]{:S(2)}) async-start(f32[8,2,128,128]{3,2,1,0:T(8,128)} %copy.99), calls=%async_computation.5 | async-start | bytes 2097152 | tf_op jit(solution)/shard_map/all_to_all | solution.py:93
  317.2 47.9 %copy-start.9 = (f32[1,512,512]{1,2,0:T(8,128)S(1)}, f32[1,512,512]{1,2,0:T(8,128)}, u32[]{:S(2)}) copy-start(f32[1,512,512]{1,2,0:T(8,128)} %all-gather.11.cloned.1.call-done) | copy-start | bytes 3145732
Sparse Core Ops, SparseCore 0:
  20.9 31.7 reduce-scatter.3
  69.4 41.6 all-gather.8
  112.7 29.4 all-gather.10
  158.0 29.3 reduce-scatter.5
  188.9 37.8 all-gather.12
  278.0 29.1 reduce-scatter.7
  308.8 46.7 all-gather.14
